TPU v7x, 32 devices: a whole 2x2x4 slice. The times are simulated.
32 devices in a mesh: owner: 4 (over y, core), rows: 8 (over z, x).
Axes of the slice: x: 2, y: 2, z: 4, core: 2. Of those that a mesh axis runs over, the one named last changes fastest.
Arguments:
- w_gate: float32 [64, 2048, 1024], P('owner', 'rows'), may hold values from -0.1875 to 0.1875
- avg_gate: float32 [64, 2048, 1024], P('owner', 'rows'), may hold values from -0.125 to 0.125
- w_up: float32 [64, 2048, 1024], P('owner', 'rows'), may hold values from -0.1875 to 0.1875
- avg_up: float32 [64, 2048, 1024], P('owner', 'rows'), may hold values from -0.125 to 0.125
- mix_share: float32 [64], P('owner'), may hold values from 0.2 to 0.8
- router_weight: float32 [2048, 64], P('rows', 'owner'), may hold values from -0.125 to 0.125
- router_gain: float32 [2048], P('rows'), may hold values from 0.25 to 1.75
Outputs:
- serve_gate: bfloat16 [64, 2048, 1024], P('owner', None, 'rows')
- serve_up: bfloat16 [64, 2048, 1024], P('owner', None, 'rows')
- scale_gate: float32 [64, 1024], P('owner', 'rows')
- scale_up: float32 [64, 1024], P('owner', 'rows')
- serve_router: bfloat16 [2048, 64], replicated
All inputs are finite; a program needn't handle non-finite values.
Results may differ from a plain program's by a relative error of at most 0.001.
Values may be sent and summed in bfloat16 or wider, within the bound.
A program may use at most 256 MiB of HBM per device.

v0:
```python
import functools

import jax
import jax.numpy as jnp
from jax import lax
from jax.experimental import pallas as pl
from jax.experimental.pallas import tpu as pltpu
from jax.sharding import PartitionSpec as P

MESH = pl.DeviceIdType.MESH
LANES = 128
STAGES = 3
STEP = 16


def plain(w_gate, avg_gate, w_up, avg_up, mix_share, router_weight, router_gain):
    fresh_gate = mix_share[:, None, None] * w_gate + (1.0 - mix_share[:, None, None]) * avg_gate
    fresh_up = mix_share[:, None, None] * w_up + (1.0 - mix_share[:, None, None]) * avg_up
    total_gate, total_up = lax.psum(
        (jnp.sum(fresh_gate * fresh_gate, axis=1), jnp.sum(fresh_up * fresh_up, axis=1)), "rows"
    )
    scale_gate = jnp.sqrt(total_gate)
    scale_up = jnp.sqrt(total_up)
    narrow_gate, narrow_up = (
        (fresh_gate / jnp.expand_dims(scale_gate, 1)).astype(jnp.bfloat16),
        (fresh_up / jnp.expand_dims(scale_up, 1)).astype(jnp.bfloat16),
    )
    serve_gate, serve_up = (
        lax.all_to_all(narrow_gate, "rows", split_axis=2, concat_axis=1, tiled=True),
        lax.all_to_all(narrow_up, "rows", split_axis=2, concat_axis=1, tiled=True),
    )
    scale_gate = lax.dynamic_slice_in_dim(
        scale_gate, lax.axis_index("rows") * serve_gate.shape[2], serve_gate.shape[2], axis=1
    )
    scale_up = lax.dynamic_slice_in_dim(
        scale_up, lax.axis_index("rows") * serve_up.shape[2], serve_up.shape[2], axis=1
    )
    part_router = (router_weight * router_gain[:, None]).astype(jnp.bfloat16)
    row_router = lax.all_gather(part_router, "rows", axis=0, tiled=True)
    serve_router = lax.all_gather(row_router, "owner", axis=1, tiled=True)
    return (serve_gate, serve_up, scale_gate, scale_up, serve_router)


def kernel(n, owners, wg, ag, wu, au, share, rw, gain,
           og, ou, sg, su, orouter,
           load, fresh, part, gotten, halves, across, held, scales, narrow, rblock,
           load_sem, rs_send, rs_recv, x_send, x_recv, ag_send, ag_recv, b_send, b_recv, own_sem, r_send, r_recv, q_send, q_recv):
    me = lax.axis_index("rows")
    mine = lax.axis_index("owner")
    experts, depth, width = wg.shape
    cols = width // n
    slots = fresh.shape[0]
    outs = (og, ou)
    order = tuple(range(n - 1, 0, -1))
    half = n // 2
    spot = lax.rem(me, half)
    top = 2 * (me // half)

    def loads(i, slot):
        return [pltpu.make_async_copy(src.at[i], load.at[slot, j], load_sem.at[slot, j])
                for j, src in enumerate((wg, ag, wu, au))]

    def rs_copy(i, d):
        peer = me ^ d
        return pltpu.make_async_remote_copy(
            src_ref=part.at[i, lax.rem(peer, half)], dst_ref=gotten.at[i, d - 1], send_sem=rs_send, recv_sem=rs_recv.at[i],
            device_id={"rows": peer}, device_id_type=MESH)

    def ag_copy(i, d):
        return pltpu.make_async_remote_copy(
            src_ref=held.at[i], dst_ref=scales.at[i, spot], send_sem=ag_send, recv_sem=ag_recv.at[i],
            device_id={"rows": me ^ d}, device_id_type=MESH)

    def cross_copy(i):
        return pltpu.make_async_remote_copy(
            src_ref=halves.at[i], dst_ref=across.at[i], send_sem=x_send, recv_sem=x_recv.at[i],
            device_id={"rows": me ^ half}, device_id_type=MESH)

    def bulk_copy(i, m, d):
        peer = me ^ d
        return pltpu.make_async_remote_copy(
            src_ref=narrow.at[m, peer, i], dst_ref=outs[m].at[i, pl.ds(me * depth, depth), :],
            send_sem=b_send.at[m, d - 1], recv_sem=b_recv.at[m, d - 1],
            device_id={"rows": peer}, device_id_type=MESH)

    def own_copy(i, m):
        return pltpu.make_async_copy(
            narrow.at[m, me, i], outs[m].at[i, pl.ds(me * depth, depth), :], own_sem.at[m])

    for copy in loads(0, 0):
        copy.start()

    barrier = pltpu.get_barrier_semaphore()
    for d in range(1, n):
        pl.semaphore_signal(barrier, inc=1, device_id={"rows": me ^ d}, device_id_type=MESH)
    for q in range(1, owners):
        pl.semaphore_signal(barrier, inc=1, device_id={"owner": mine ^ q}, device_id_type=MESH)

    rexp, rlen = rw.shape
    rrows = pl.ds(pl.multiple_of(mine * rexp, rexp), rexp)
    rcols = pl.ds(pl.multiple_of(me * rlen, LANES), rlen)
    rblock[...] = (rw[...] * gain[...]).astype(jnp.bfloat16)

    def router_copy(d):
        return pltpu.make_async_remote_copy(
            src_ref=rblock, dst_ref=orouter.at[rrows, rcols], send_sem=r_send.at[d - 1], recv_sem=r_recv,
            device_id={"rows": me ^ d}, device_id_type=MESH)

    def router_across(q):
        return pltpu.make_async_remote_copy(
            src_ref=orouter.at[rrows, :], dst_ref=orouter.at[rrows, :], send_sem=q_send.at[q - 1],
            recv_sem=q_recv.at[q - 1], device_id={"owner": mine ^ q}, device_id_type=MESH)

    orouter[rrows, rcols] = rblock[...]

    def mix(i):
        slot = i % 2 if isinstance(i, int) else lax.rem(i, 2)
        fslot = i if isinstance(i, int) else lax.rem(i, slots)
        a = share[i]
        b = 1.0 - a
        for copy in loads(i, slot):
            copy.wait()
        if isinstance(i, int):
            for copy in loads(1, 1):
                copy.start()
        for m in range(2):
            def rows_step(t, acc):
                rows = pl.ds(pl.multiple_of(t * STEP, STEP), STEP)
                f = a * load[slot, 2 * m, rows, :] + b * load[slot, 2 * m + 1, rows, :]
                fresh[fslot, m, rows, :] = f
                f = f * f
                for r in range(0, STEP, 8):
                    acc = acc + f[r:r + 8]
                return acc
            acc = lax.fori_loop(0, depth // STEP, rows_step, jnp.zeros((8, width), jnp.float32))
            total = jnp.sum(acc, axis=0, keepdims=True)
            for c in range(n):
                part[i, c % half, pl.ds(2 * (c // half) + m, 1), :] = total[:, c * cols:(c + 1) * cols]

        if isinstance(i, int):
            for copy in loads(i + 2, slot):
                copy.start()
        else:
            @pl.when(i + 2 < experts)
            def _():
                for copy in loads(i + 2, slot):
                    copy.start()

    def spread(i):
        for d in range(half - 1, 0, -1):
            rs_copy(i, d).start()

    def halve(i):
        pltpu.make_async_copy(gotten.at[i], gotten.at[i], rs_recv.at[i]).wait()
        total = part[i, spot]
        for d in range(half - 1):
            total = total + gotten[i, d]
        halves[i] = total
        cross_copy(i).start()

    def settle(i):
        cross_copy(i).wait_recv()
        scale = jnp.sqrt(halves[i] + across[i])
        held[i] = scale
        scales[i, spot] = scale
        sg[pl.ds(i, 1), :] = held[i, pl.ds(top, 1), :]
        su[pl.ds(i, 1), :] = held[i, pl.ds(top + 1, 1), :]
        for d in range(half - 1, 0, -1):
            ag_copy(i, d).start()

    def send(i):
        fslot = lax.rem(i, slots)
        landed = scales.at[i, pl.ds(0, half - 1)]
        pltpu.make_async_copy(landed, landed, ag_recv.at[i]).wait()
        for m in range(2):
            inverse = [1.0 / scales[i, c % half, pl.ds(2 * (c // half) + m, 1), :] for c in range(n)]

            def rows_step(t, carry):
                rows = pl.ds(pl.multiple_of(t * STEP, STEP), STEP)
                for c in range(n):
                    f = fresh[fslot, m, rows, c * cols:(c + 1) * cols]
                    narrow[m, c, i, rows, :] = (f * inverse[c]).astype(jnp.bfloat16)
                return carry
            lax.fori_loop(0, depth // STEP, rows_step, 0)
        for d in order:
            for m in range(2):
                bulk_copy(i, m, d).start()
        for m in range(2):
            own_copy(i, m).start()

    def turn(i, carry):
        @pl.when(i < experts)
        def _():
            mix(i)
            spread(i)

        @pl.when(i <= experts)
        def _():
            halve(i - 1)

        @pl.when((i >= 2) & (i <= experts + 1))
        def _():
            settle(i - 2)

        @pl.when(i >= STAGES)
        def _():
            send(i - STAGES)

        @pl.when(i == STAGES)
        def _():
            for d in order:
                router_copy(d).start()
        return carry

    mix(0)
    pl.semaphore_wait(barrier, n + owners - 2)
    spread(0)
    lax.fori_loop(1, experts + STAGES, turn, 0)

    got = orouter.at[rrows, pl.ds(0, (n - 1) * rlen)]
    pltpu.make_async_copy(got, got, r_recv).wait()
    for q in range(1, owners):
        router_across(q).start()
    for d in range(1, n):
        router_copy(d).wait_send()
    for m in range(2):
        block = outs[m].at[:, pl.ds(0, depth), :]
        pltpu.make_async_copy(block, block, own_sem.at[m]).wait()
        for d in range(1, n):
            pltpu.make_async_copy(block, block, b_send.at[m, d - 1]).wait()
            pltpu.make_async_copy(block, block, b_recv.at[m, d - 1]).wait()
    pltpu.make_async_copy(gotten, gotten, rs_send).wait()
    pltpu.make_async_copy(across, across, x_send).wait()
    every = scales.at[:, pl.ds(0, half - 1)]
    pltpu.make_async_copy(every, every, ag_send).wait()
    for q in range(1, owners):
        router_across(q).wait()


def body(n, owners, w_gate, avg_gate, w_up, avg_up, mix_share, router_weight, router_gain):
    experts, depth, width = w_gate.shape
    cols = width // n
    rlen, rexp = router_weight.shape
    f32, bf16 = jnp.float32, jnp.bfloat16
    dma = pltpu.SemaphoreType.DMA
    hbm = pl.BlockSpec(memory_space=pl.ANY)
    vmem = pl.BlockSpec(memory_space=pltpu.VMEM)
    smem = pl.BlockSpec(memory_space=pltpu.SMEM)
    serve_gate, serve_up, scale_gate, scale_up, router = pl.pallas_call(
        functools.partial(kernel, n, owners),
        out_shape=(
            OUT((experts, n * depth, cols), bf16),
            OUT((experts, n * depth, cols), bf16),
            OUT((experts, cols), f32),
            OUT((experts, cols), f32),
            OUT((owners * rexp, n * rlen), bf16),
        ),
        in_specs=[hbm] * 4 + [smem, vmem, vmem],
        out_specs=(OUT_SPEC, OUT_SPEC, vmem, vmem, vmem),
        scratch_shapes=[
            pltpu.VMEM((2, 4, depth, width), f32),
            pltpu.VMEM((STAGES + 1, 2, depth, width), f32),
            pltpu.VMEM((experts, n // 2, 4, cols), f32),
            pltpu.VMEM((experts, n // 2 - 1, 4, cols), f32),
            pltpu.VMEM((experts, 4, cols), f32),
            pltpu.VMEM((experts, 4, cols), f32),
            pltpu.VMEM((experts, 4, cols), f32),
            pltpu.VMEM((experts, n // 2, 4, cols), f32),
            pltpu.VMEM((2, n, experts, depth, cols), bf16),
            pltpu.VMEM((rexp, rlen), bf16),
            dma((2, 4)), dma, dma((experts,)), dma, dma((experts,)), dma, dma((experts,)),
            dma((2, n - 1)), dma((2, n - 1)), dma((2,)),
            dma((n - 1,)), dma, dma((owners - 1,)), dma((owners - 1,)),
        ],
        compiler_params=pltpu.CompilerParams(
            collective_id=0, has_side_effects=True, vmem_limit_bytes=LIMIT
        ),
    )(w_gate, avg_gate, w_up, avg_up, mix_share, router_weight.T, router_gain[None, :])
    return serve_gate, serve_up, scale_gate, scale_up, router.T


OUT = pltpu.VMEM
OUT_SPEC = pl.BlockSpec(memory_space=pltpu.VMEM)
LIMIT = 44 * 1024 * 1024


def fits(mesh, w_gate, router_weight):
    n, owners = mesh.shape["rows"], mesh.shape["owner"]
    experts, depth, width = w_gate.shape[0] // owners, w_gate.shape[1] // n, w_gate.shape[2]
    need = 4 * depth * width * (8 + 2 * (STAGES + 1)) + 4 * experts * depth * width
    return (
        n > 2 and owners > 1 and n & (n - 1) == 0 and owners & (owners - 1) == 0
        and width % (n * LANES) == 0 and depth % LANES == 0 and depth % STEP == 0
        and experts % 16 == 0 and (router_weight.shape[1] // owners) % 16 == 0
        and need < 40 * 1024 * 1024
    )


def solution(mesh):
    in_specs = (
        P("owner", "rows", None),
        P("owner", "rows", None),
        P("owner", "rows", None),
        P("owner", "rows", None),
        P("owner"),
        P("rows", "owner"),
        P("rows"),
    )
    out_specs = (
        P("owner", None, "rows"),
        P("owner", None, "rows"),
        P("owner", "rows"),
        P("owner", "rows"),
        P(),
    )

    def call(w_gate, avg_gate, w_up, avg_up, mix_share, router_weight, router_gain):
        inner = plain
        if fits(mesh, w_gate, router_weight):
            inner = functools.partial(body, mesh.shape["rows"], mesh.shape["owner"])
        step = jax.shard_map(inner, mesh=mesh, in_specs=in_specs, out_specs=out_specs, check_vma=False)
        return step(w_gate, avg_gate, w_up, avg_up, mix_share, router_weight, router_gain)

    return call
```

profile of v0, /device:TPU:0, one launch (start us, length us, event | category | flops | bytes accessed | tf_op | source)
XLA Modules:
  0.0 388.8 jit_solution(7426619054454149087)
XLA Ops:
  0.6 379.4 %shard_map.110 = (bf16[16,2048,128]{2,1,0:T(8,128)(2,1)S(1)}, bf16[16,2048,128]{2,1,0:T(8,128)(2,1)S(1)}, f32[16,128]{1,0:T(8,128)S(1)}, f32[16,128]{1,0:T(8,128)S(1)}, bf16[64,2048]{1,0:T(8,128)(2,1)S(1)}) custom-call(f32[16,256,1024]{2,1,0:T(8,128)} %wg.1, f32[16,256,1024]{2,1,0:T(8,128)} %ag.1, f32[16,256,1024]{2,1,0:T(8,128)} %wu.1, ...), custom_call_target="tpu_custom_call" | custom-call | tf_op jit(solution)/shard_map/pallas_call | solution.py:249
  380.1 3.4 copy.17
  383.5 0.6 copy.19
  384.1 0.6 copy.20
  384.7 0.7 copy.21
  385.4 3.4 copy.18
where the time goes:
time: 389 us
  Pallas kernels  379 us (97%)
  local copies, waits for them, and re-layouts  8.69 us (2%)
    pallas_call x1, Pallas kernels, body(): pl.pallas_call(functools.partial(kernel, n, owners), out_shape=(OUT((expe...  379 us
    unnamed x5, local copies, waits for them, and re-layouts  8.69 us

commit v1 on v0

--- a/solution.py
+++ b/solution.py
@@ -11,6 +11,8 @@
 LANES = 128
 STAGES = 3
 STEP = 16
+PIECES = 4
+HEAD = (4, 4, 2)
 
 
 def plain(w_gate, avg_gate, w_up, avg_up, mix_share, router_weight, router_gain):
@@ -44,22 +46,41 @@
 def kernel(n, owners, wg, ag, wu, au, share, rw, gain,
            og, ou, sg, su, orouter,
            load, fresh, part, gotten, halves, across, held, scales, narrow, rblock,
-           load_sem, rs_send, rs_recv, x_send, x_recv, ag_send, ag_recv, b_send, b_recv, own_sem, r_send, r_recv, q_send, q_recv):
+           load_sem, head_sem, raw_send, raw_recv, rest_send, rest_recv, rs_send, rs_recv, x_send, x_recv, ag_send, ag_recv, b_send, b_recv, own_sem, r_send, r_recv, q_send, q_recv):
     me = lax.axis_index("rows")
     mine = lax.axis_index("owner")
     experts, depth, width = wg.shape
     cols = width // n
     slots = fresh.shape[0]
     outs = (og, ou)
-    order = tuple(range(n - 1, 0, -1))
     half = n // 2
+    order = tuple(range(half, n)) + tuple(range(half - 1, 0, -1))
     spot = lax.rem(me, half)
     top = 2 * (me // half)
+    near = half * (me // half)
+    far = half - near
+    raws = len(HEAD) - 1
+    head = [depth // k for k in HEAD]
+    edges = [sum(head[:p]) for p in range(len(head))]
+    raw = edges[raws]
 
     def loads(i, slot):
         return [pltpu.make_async_copy(src.at[i], load.at[slot, j], load_sem.at[slot, j])
                 for j, src in enumerate((wg, ag, wu, au))]
 
+    def head_loads(p):
+        rows = pl.ds(edges[p], head[p])
+        return [pltpu.make_async_copy(src.at[0, rows], load.at[0, j, rows], head_sem.at[p, j])
+                for j, src in enumerate((wg, ag, wu, au))]
+
+    def raw_copy(p, m, d):
+        peer = me ^ d
+        rows = pl.ds(edges[p], head[p])
+        there = pl.ds(pl.multiple_of(me * depth + edges[p], STEP), head[p])
+        return pltpu.make_async_remote_copy(
+            src_ref=narrow.at[m, peer, 0, rows], dst_ref=outs[m].at[0, there, :], send_sem=raw_send, recv_sem=raw_recv,
+            device_id={"rows": peer}, device_id_type=MESH)
+
     def rs_copy(i, d):
         peer = me ^ d
         return pltpu.make_async_remote_copy(
@@ -83,12 +104,21 @@
             send_sem=b_send.at[m, d - 1], recv_sem=b_recv.at[m, d - 1],
             device_id={"rows": peer}, device_id_type=MESH)
 
+    def rest_copy(m, d):
+        peer = me ^ d
+        there = pl.ds(pl.multiple_of(me * depth + raw, STEP), depth - raw)
+        return pltpu.make_async_remote_copy(
+            src_ref=narrow.at[m, peer, 0, pl.ds(raw, depth - raw)], dst_ref=outs[m].at[0, there, :],
+            send_sem=rest_send, recv_sem=rest_recv,
+            device_id={"rows": peer}, device_id_type=MESH)
+
     def own_copy(i, m):
         return pltpu.make_async_copy(
             narrow.at[m, me, i], outs[m].at[i, pl.ds(me * depth, depth), :], own_sem.at[m])
 
-    for copy in loads(0, 0):
-        copy.start()
+    for p in range(len(HEAD)):
+        for copy in head_loads(p):
+            copy.start()
 
     barrier = pltpu.get_barrier_semaphore()
     for d in range(1, n):
@@ -113,38 +143,47 @@
 
     orouter[rrows, rcols] = rblock[...]
 
-    def mix(i):
-        slot = i % 2 if isinstance(i, int) else lax.rem(i, 2)
-        fslot = i if isinstance(i, int) else lax.rem(i, slots)
+    def blend(i, slot, fslot, m, lo, hi, acc, ship=False):
         a = share[i]
         b = 1.0 - a
+
+        def rows_step(t, acc):
+            rows = pl.ds(pl.multiple_of(t * STEP, STEP), STEP)
+            f = a * load[slot, 2 * m, rows, :] + b * load[slot, 2 * m + 1, rows, :]
+            fresh[fslot, m, rows, :] = f
+            f = f * f
+            for r in range(0, STEP, 8):
+                acc = acc + f[r:r + 8]
+            if ship:
+                for j in range(half):
+                    c = far + j
+                    g = fresh[fslot, m, rows, pl.ds(pl.multiple_of(c * cols, LANES), cols)]
+                    narrow[m, c, 0, rows, :] = g.astype(jnp.bfloat16)
+            return acc
+        return lax.fori_loop(lo // STEP, hi // STEP, rows_step, acc)
+
+    def sums(i, m, acc):
+        total = jnp.sum(acc, axis=0, keepdims=True)
+        for c in range(n):
+            part[i, c % half, pl.ds(2 * (c // half) + m, 1), :] = total[:, c * cols:(c + 1) * cols]
+
+    def mix(i):
+        slot = lax.rem(i, 2)
         for copy in loads(i, slot):
             copy.wait()
-        if isinstance(i, int):
-            for copy in loads(1, 1):
-                copy.start()
         for m in range(2):
-            def rows_step(t, acc):
-                rows = pl.ds(pl.multiple_of(t * STEP, STEP), STEP)
-                f = a * load[slot, 2 * m, rows, :] + b * load[slot, 2 * m + 1, rows, :]
-                fresh[fslot, m, rows, :] = f
-                f = f * f
-                for r in range(0, STEP, 8):
-                    acc = acc + f[r:r + 8]
-                return acc
-            acc = lax.fori_loop(0, depth // STEP, rows_step, jnp.zeros((8, width), jnp.float32))
-            total = jnp.sum(acc, axis=0, keepdims=True)
-            for c in range(n):
-                part[i, c % half, pl.ds(2 * (c // half) + m, 1), :] = total[:, c * cols:(c + 1) * cols]
-
-        if isinstance(i, int):
+            sums(i, m, blend(i, slot, lax.rem(i, slots), m, 0, depth, jnp.zeros((8, width), jnp.float32)))
+
+        @pl.when(i + 2 < experts)
+        def _():
             for copy in loads(i + 2, slot):
                 copy.start()
-        else:
-            @pl.when(i + 2 < experts)
-            def _():
-                for copy in loads(i + 2, slot):
-                    copy.start()
+
+    def ship(p):
+        for d in order:
+            if d >= half:
+                for m in range(2):
+                    raw_copy(p, m, d).start()
 
     def spread(i):
         for d in range(half - 1, 0, -1):
@@ -188,6 +227,37 @@
         for m in range(2):
             own_copy(i, m).start()
 
+    def scaled(i, m, c, rows, col, inverse):
+        f = fresh[lax.rem(i, slots), m, rows, pl.ds(col, cols)]
+        narrow[m, c, i, rows, :] = (f * inverse).astype(jnp.bfloat16)
+
+    def send_first():
+        landed = scales.at[0, pl.ds(0, half - 1)]
+        pltpu.make_async_copy(landed, landed, ag_recv.at[0]).wait()
+        for m in range(2):
+            def near_step(t, carry):
+                rows = pl.ds(pl.multiple_of(t * STEP, STEP), STEP)
+                for j in range(half):
+                    c = near + j
+                    scaled(0, m, c, rows, pl.multiple_of(c * cols, LANES), 1.0 / scales[0, j, pl.ds(top + m, 1), :])
+                return carry
+            lax.fori_loop(0, raw // STEP, near_step, 0)
+
+            def rows_step(t, carry):
+                rows = pl.ds(pl.multiple_of(t * STEP, STEP), STEP)
+                for c in range(n):
+                    scaled(0, m, c, rows, c * cols, 1.0 / scales[0, c % half, pl.ds(2 * (c // half) + m, 1), :])
+                return carry
+            lax.fori_loop(raw // STEP, depth // STEP, rows_step, 0)
+        for d in order:
+            for m in range(2):
+                if d < half:
+                    bulk_copy(0, m, d).start()
+                else:
+                    rest_copy(m, d).start()
+        for m in range(2):
+            own_copy(0, m).start()
+
     def turn(i, carry):
         @pl.when(i < experts)
         def _():
@@ -198,24 +268,54 @@
         def _():
             halve(i - 1)
 
-        @pl.when((i >= 2) & (i <= experts + 1))
-        def _():
-            settle(i - 2)
-
-        @pl.when(i >= STAGES)
-        def _():
-            send(i - STAGES)
-
-        @pl.when(i == STAGES)
-        def _():
+        @pl.when(i == 1)
+        def _():
+            for p in range(1, raws):
+                ship(p)
             for d in order:
                 router_copy(d).start()
+
+        @pl.when((i >= 2) & (i <= experts + 1))
+        def _():
+            settle(i - 2)
+
+        @pl.when(i == STAGES)
+        def _():
+            send_first()
+
+        @pl.when(i > STAGES)
+        def _():
+            send(i - STAGES)
         return carry
 
-    mix(0)
-    pl.semaphore_wait(barrier, n + owners - 2)
+    accs = [jnp.zeros((8, width), jnp.float32)] * 2
+    for p in range(len(HEAD)):
+        for copy in head_loads(p):
+            copy.wait()
+        accs = [blend(0, 0, 0, m, edges[p], edges[p] + head[p], accs[m], p < raws) for m in range(2)]
+        if p == 0:
+            for copy in loads(1, 1):
+                copy.start()
+            pl.semaphore_wait(barrier, n + owners - 2)
+            ship(0)
+    for m in range(2):
+        sums(0, m, accs[m])
     spread(0)
+    for copy in loads(2, 0):
+        copy.start()
     lax.fori_loop(1, experts + STAGES, turn, 0)
+
+    early = og.at[0, pl.ds(0, 2 * half * raw), :]
+    pltpu.make_async_copy(early, early, raw_recv).wait()
+    for m in range(2):
+        inverse = 1.0 / held[0, pl.ds(top + m, 1), :]
+
+        def fix(t, carry):
+            for j in range(half):
+                rows = pl.ds(pl.multiple_of((far + j) * depth + t * STEP, STEP), STEP)
+                outs[m][0, rows, :] = (outs[m][0, rows, :].astype(jnp.float32) * inverse).astype(jnp.bfloat16)
+            return carry
+        lax.fori_loop(0, raw // STEP, fix, 0)
 
     got = orouter.at[rrows, pl.ds(0, (n - 1) * rlen)]
     pltpu.make_async_copy(got, got, r_recv).wait()
@@ -226,15 +326,36 @@
     for m in range(2):
         block = outs[m].at[:, pl.ds(0, depth), :]
         pltpu.make_async_copy(block, block, own_sem.at[m]).wait()
+        most = outs[m].at[pl.ds(0, experts - 1), pl.ds(0, depth), :]
         for d in range(1, n):
-            pltpu.make_async_copy(block, block, b_send.at[m, d - 1]).wait()
-            pltpu.make_async_copy(block, block, b_recv.at[m, d - 1]).wait()
+            sent = block if d < half else most
+            pltpu.make_async_copy(sent, sent, b_send.at[m, d - 1]).wait()
+            pltpu.make_async_copy(sent, sent, b_recv.at[m, d - 1]).wait()
+    pltpu.make_async_copy(early, early, raw_send).wait()
+    rest = og.at[0, pl.ds(0, 2 * half * (depth - raw)), :]
+    pltpu.make_async_copy(rest, rest, rest_send).wait()
+    pltpu.make_async_copy(rest, rest, rest_recv).wait()
     pltpu.make_async_copy(gotten, gotten, rs_send).wait()
     pltpu.make_async_copy(across, across, x_send).wait()
     every = scales.at[:, pl.ds(0, half - 1)]
     pltpu.make_async_copy(every, every, ag_send).wait()
     for q in range(1, owners):
         router_across(q).wait()
+
+
+def flush(*refs):
+    sources, targets, sem = refs[:len(refs) // 2], refs[len(refs) // 2:-1], refs[-1]
+    copies = []
+    for source, target in zip(sources, targets):
+        pieces = PIECES if len(source.shape) == 3 else 1
+        size = source.shape[0] // pieces
+        for p in range(pieces):
+            block = pl.ds(p * size, size)
+            copies.append(pltpu.make_async_copy(source.at[block], target.at[block], sem.at[len(copies)]))
+    for copy in copies:
+        copy.start()
+    for copy in copies:
+        copy.wait()
 
 
 def body(n, owners, w_gate, avg_gate, w_up, avg_up, mix_share, router_weight, router_gain):
@@ -246,7 +367,7 @@
     hbm = pl.BlockSpec(memory_space=pl.ANY)
     vmem = pl.BlockSpec(memory_space=pltpu.VMEM)
     smem = pl.BlockSpec(memory_space=pltpu.SMEM)
-    serve_gate, serve_up, scale_gate, scale_up, router = pl.pallas_call(
+    landed = pl.pallas_call(
         functools.partial(kernel, n, owners),
         out_shape=(
             OUT((experts, n * depth, cols), bf16),
@@ -268,7 +389,7 @@
             pltpu.VMEM((experts, n // 2, 4, cols), f32),
             pltpu.VMEM((2, n, experts, depth, cols), bf16),
             pltpu.VMEM((rexp, rlen), bf16),
-            dma((2, 4)), dma, dma((experts,)), dma, dma((experts,)), dma, dma((experts,)),
+            dma((2, 4)), dma((len(HEAD), 4)), dma, dma, dma, dma, dma, dma((experts,)), dma, dma((experts,)), dma, dma((experts,)),
             dma((2, n - 1)), dma((2, n - 1)), dma((2,)),
             dma((n - 1,)), dma, dma((owners - 1,)), dma((owners - 1,)),
         ],
@@ -276,6 +397,14 @@
             collective_id=0, has_side_effects=True, vmem_limit_bytes=LIMIT
         ),
     )(w_gate, avg_gate, w_up, avg_up, mix_share, router_weight.T, router_gain[None, :])
+    serve_gate, serve_up, scale_gate, scale_up, router = pl.pallas_call(
+        flush,
+        out_shape=[pltpu.HBM(x.shape, x.dtype) for x in landed],
+        in_specs=[vmem] * len(landed),
+        out_specs=[pl.BlockSpec(memory_space=pltpu.HBM)] * len(landed),
+        scratch_shapes=[dma((len(landed) + 2 * (PIECES - 1),))],
+        compiler_params=pltpu.CompilerParams(vmem_limit_bytes=1024 * 1024),
+    )(*landed)
     return serve_gate, serve_up, scale_gate, scale_up, router.T
 
 
@@ -287,12 +416,14 @@
 def fits(mesh, w_gate, router_weight):
     n, owners = mesh.shape["rows"], mesh.shape["owner"]
     experts, depth, width = w_gate.shape[0] // owners, w_gate.shape[1] // n, w_gate.shape[2]
+    head = [depth // k for k in HEAD]
+    half_raw = n // 2 * sum(head[:-1])
     need = 4 * depth * width * (8 + 2 * (STAGES + 1)) + 4 * experts * depth * width
     return (
         n > 2 and owners > 1 and n & (n - 1) == 0 and owners & (owners - 1) == 0
         and width % (n * LANES) == 0 and depth % LANES == 0 and depth % STEP == 0
         and experts % 16 == 0 and (router_weight.shape[1] // owners) % 16 == 0
-        and need < 40 * 1024 * 1024
+        and depth == sum(head) and head[0] % STEP == 0 and 64 * half_raw <= experts * depth * n and need < 40 * 1024 * 1024
     )
 
 

time: 389 us -> 378 us (0.972)
  local copies, waits for them, and re-layouts: 8.69 us -> 0 us
  Pallas kernels: 379 us -> 375 us
    pallas_call x1, Pallas kernels: 379 us -> 369 us  [body(): pl.pallas_call(functools.partial(kernel, n, owners), out_shape=(OUT((expe...]
    unnamed x5 -> x0, local copies, waits for them, and re-layouts: 8.69 us -> none
    pallas_call x0 -> x1, Pallas kernels: none -> 5.98 us  [body(): pl.pallas_call(flush, out_shape=[pltpu.HBM(x.shape, x.dtype) for x in lan...]
where the time goes in v1:
time: 378 us; the launch traced here: 376 us
  Pallas kernels  375 us (99%)
    pallas_call x1, Pallas kernels, body(): pl.pallas_call(functools.partial(kernel, n, owners), out_shape=(OUT((expe...  369 us

profile of v1, /device:TPU:0, one launch (start us, length us, event | category | flops | bytes accessed | tf_op | source)
XLA Modules:
  0.0 376.0 jit_solution(16683113780651769075)
XLA Ops:
  0.6 369.4 %shard_map.110 = (bf16[16,2048,128]{2,1,0:T(8,128)(2,1)S(1)}, bf16[16,2048,128]{2,1,0:T(8,128)(2,1)S(1)}, f32[16,128]{1,0:T(8,128)S(1)}, f32[16,128]{1,0:T(8,128)S(1)}, bf16[64,2048]{1,0:T(8,128)(2,1)S(1)}) custom-call(f32[16,256,1024]{2,1,0:T(8,128)} %wg.1, f32[16,256,1024]{2,1,0:T(8,128)} %ag.1, f32[16,256,1024]{2,1,0:T(8,128)} %wu.1, ...), custom_call_target="tpu_custom_call" | custom-call | tf_op jit(solution)/shard_map/pallas_call | solution.py:370
  370.0 6.0 %shard_map.111 = (bf16[16,2048,128]{2,1,0:T(8,128)(2,1)}, bf16[16,2048,128]{2,1,0:T(8,128)(2,1)}, f32[16,128]{1,0:T(8,128)}, f32[16,128]{1,0:T(8,128)}, bf16[64,2048]{1,0:T(8,128)(2,1)}) custom-call(bf16[16,2048,128]{2,1,0:T(8,128)(2,1)S(1)} %get-tuple-element.15.refs_0_, bf16[16,2048,128]{2,1,0:T(8,128)(2,1)S(1)} %get-tuple-element.16.refs_1_, ...), custom_call_target="tpu_custom_call" | custom-call | tf_op jit(solution)/shard_map/pallas_call | solution.py:400

commit v2 on v1

--- a/solution.py
+++ b/solution.py
@@ -9,10 +9,11 @@
 
 MESH = pl.DeviceIdType.MESH
 LANES = 128
-STAGES = 3
+SLOTS = 5
+LEAD = 2
 STEP = 16
 PIECES = 4
-HEAD = (4, 4, 2)
+HEAD = (8, 8, 4, 2)
 
 
 def plain(w_gate, avg_gate, w_up, avg_up, mix_share, router_weight, router_gain):
@@ -43,10 +44,10 @@
     return (serve_gate, serve_up, scale_gate, scale_up, serve_router)
 
 
-def kernel(n, owners, wg, ag, wu, au, share, rw, gain,
+def kernel(n, owners, wg, ag, wu, au, share_in, rw_in, gain_in,
            og, ou, sg, su, orouter,
-           load, fresh, part, gotten, halves, across, held, scales, narrow, rblock,
-           load_sem, head_sem, raw_send, raw_recv, rest_send, rest_recv, rs_send, rs_recv, x_send, x_recv, ag_send, ag_recv, b_send, b_recv, own_sem, r_send, r_recv, q_send, q_recv):
+           load, fresh, part, gotten, halves, across, held, scales, narrow, rblock, share, rw, gain,
+           small_sem, load_sem, head_sem, raw_send, raw_recv, rest_send, rest_recv, rs_send, rs_recv, x_send, x_recv, ag_send, ag_recv, b_send, b_recv, own_sem, r_send, r_recv, f_send, f_recv, q_send, q_recv):
     me = lax.axis_index("rows")
     mine = lax.axis_index("owner")
     experts, depth, width = wg.shape
@@ -92,9 +93,10 @@
             src_ref=held.at[i], dst_ref=scales.at[i, spot], send_sem=ag_send, recv_sem=ag_recv.at[i],
             device_id={"rows": me ^ d}, device_id_type=MESH)
 
-    def cross_copy(i):
-        return pltpu.make_async_remote_copy(
-            src_ref=halves.at[i], dst_ref=across.at[i], send_sem=x_send, recv_sem=x_recv.at[i],
+    def cross_copy(i, count):
+        block = pl.ds(i, count)
+        return pltpu.make_async_remote_copy(
+            src_ref=halves.at[block], dst_ref=across.at[block], send_sem=x_send, recv_sem=x_recv.at[i],
             device_id={"rows": me ^ half}, device_id_type=MESH)
 
     def bulk_copy(i, m, d):
@@ -116,9 +118,14 @@
         return pltpu.make_async_copy(
             narrow.at[m, me, i], outs[m].at[i, pl.ds(me * depth, depth), :], own_sem.at[m])
 
+    smalls = [pltpu.make_async_copy(src, dst, small_sem.at[j])
+              for j, (src, dst) in enumerate(((share_in, share), (rw_in, rw), (gain_in, gain)))]
+    smalls[0].start()
     for p in range(len(HEAD)):
         for copy in head_loads(p):
             copy.start()
+    for copy in smalls[1:]:
+        copy.start()
 
     barrier = pltpu.get_barrier_semaphore()
     for d in range(1, n):
@@ -126,14 +133,19 @@
     for q in range(1, owners):
         pl.semaphore_signal(barrier, inc=1, device_id={"owner": mine ^ q}, device_id_type=MESH)
 
-    rexp, rlen = rw.shape
+    rexp, rlen = rw_in.shape
     rrows = pl.ds(pl.multiple_of(mine * rexp, rexp), rexp)
     rcols = pl.ds(pl.multiple_of(me * rlen, LANES), rlen)
-    rblock[...] = (rw[...] * gain[...]).astype(jnp.bfloat16)
 
     def router_copy(d):
         return pltpu.make_async_remote_copy(
-            src_ref=rblock, dst_ref=orouter.at[rrows, rcols], send_sem=r_send.at[d - 1], recv_sem=r_recv,
+            src_ref=rblock, dst_ref=orouter.at[rrows, rcols], send_sem=r_send, recv_sem=r_recv.at[d // half],
+            device_id={"rows": me ^ d}, device_id_type=MESH)
+
+    def router_forward(d):
+        block = orouter.at[rrows, pl.ds(pl.multiple_of((me ^ half) * rlen, LANES), rlen)]
+        return pltpu.make_async_remote_copy(
+            src_ref=block, dst_ref=block, send_sem=f_send, recv_sem=f_recv,
             device_id={"rows": me ^ d}, device_id_type=MESH)
 
     def router_across(q):
@@ -141,7 +153,11 @@
             src_ref=orouter.at[rrows, :], dst_ref=orouter.at[rrows, :], send_sem=q_send.at[q - 1],
             recv_sem=q_recv.at[q - 1], device_id={"owner": mine ^ q}, device_id_type=MESH)
 
-    orouter[rrows, rcols] = rblock[...]
+    def gate_rows():
+        for copy in smalls[1:]:
+            copy.wait()
+        rblock[...] = (rw[...] * gain[...]).astype(jnp.bfloat16)
+        orouter[rrows, rcols] = rblock[...]
 
     def blend(i, slot, fslot, m, lo, hi, acc, ship=False):
         a = share[i]
@@ -180,10 +196,9 @@
                 copy.start()
 
     def ship(p):
-        for d in order:
-            if d >= half:
-                for m in range(2):
-                    raw_copy(p, m, d).start()
+        for m in range(2):
+            for d in range(half, n):
+                raw_copy(p, m, d).start()
 
     def spread(i):
         for d in range(half - 1, 0, -1):
@@ -195,10 +210,23 @@
         for d in range(half - 1):
             total = total + gotten[i, d]
         halves[i] = total
-        cross_copy(i).start()
+
+        @pl.when(i < LEAD)
+        def _():
+            cross_copy(i, 1).start()
+
+        @pl.when((i >= LEAD) & (lax.rem(i, 2) == 1))
+        def _():
+            cross_copy(i - 1, 2).start()
 
     def settle(i):
-        cross_copy(i).wait_recv()
+        @pl.when(i < LEAD)
+        def _():
+            cross_copy(i, 1).wait_recv()
+
+        @pl.when((i >= LEAD) & (lax.rem(i, 2) == 0))
+        def _():
+            cross_copy(i, 2).wait_recv()
         scale = jnp.sqrt(halves[i] + across[i])
         held[i] = scale
         scales[i, spot] = scale
@@ -221,10 +249,8 @@
                     narrow[m, c, i, rows, :] = (f * inverse[c]).astype(jnp.bfloat16)
                 return carry
             lax.fori_loop(0, depth // STEP, rows_step, 0)
-        for d in order:
-            for m in range(2):
+            for d in order:
                 bulk_copy(i, m, d).start()
-        for m in range(2):
             own_copy(i, m).start()
 
     def scaled(i, m, c, rows, col, inverse):
@@ -249,13 +275,8 @@
                     scaled(0, m, c, rows, c * cols, 1.0 / scales[0, c % half, pl.ds(2 * (c // half) + m, 1), :])
                 return carry
             lax.fori_loop(raw // STEP, depth // STEP, rows_step, 0)
-        for d in order:
-            for m in range(2):
-                if d < half:
-                    bulk_copy(0, m, d).start()
-                else:
-                    rest_copy(m, d).start()
-        for m in range(2):
+            for d in order:
+                (bulk_copy(0, m, d) if d < half else rest_copy(m, d)).start()
             own_copy(0, m).start()
 
     def turn(i, carry):
@@ -272,22 +293,39 @@
         def _():
             for p in range(1, raws):
                 ship(p)
-            for d in order:
+            gate_rows()
+            for d in range(half, 0, -1):
                 router_copy(d).start()
 
-        @pl.when((i >= 2) & (i <= experts + 1))
+        @pl.when((i >= 2) & (i < LEAD + 2))
         def _():
             settle(i - 2)
 
-        @pl.when(i == STAGES)
+        @pl.when((i >= LEAD + 3) & (i <= experts + 2))
+        def _():
+            settle(i - 3)
+
+        @pl.when(i == 3)
         def _():
             send_first()
 
-        @pl.when(i > STAGES)
-        def _():
-            send(i - STAGES)
+        @pl.when((i > 3) & (i < LEAD + 3))
+        def _():
+            send(i - 3)
+
+        @pl.when(i >= LEAD + 4)
+        def _():
+            send(i - 4)
+
+        @pl.when(i == LEAD + 4)
+        def _():
+            got = orouter.at[rrows, pl.ds(0, rlen)]
+            pltpu.make_async_copy(got, got, r_recv.at[1]).wait()
+            for d in range(half - 1, 0, -1):
+                router_forward(d).start()
         return carry
 
+    smalls[0].wait()
     accs = [jnp.zeros((8, width), jnp.float32)] * 2
     for p in range(len(HEAD)):
         for copy in head_loads(p):
@@ -303,7 +341,7 @@
     spread(0)
     for copy in loads(2, 0):
         copy.start()
-    lax.fori_loop(1, experts + STAGES, turn, 0)
+    lax.fori_loop(1, experts + 4, turn, 0)
 
     early = og.at[0, pl.ds(0, 2 * half * raw), :]
     pltpu.make_async_copy(early, early, raw_recv).wait()
@@ -317,12 +355,14 @@
             return carry
         lax.fori_loop(0, raw // STEP, fix, 0)
 
-    got = orouter.at[rrows, pl.ds(0, (n - 1) * rlen)]
-    pltpu.make_async_copy(got, got, r_recv).wait()
+    got = orouter.at[rrows, pl.ds(0, (half - 1) * rlen)]
+    pltpu.make_async_copy(got, got, r_recv.at[0]).wait()
+    pltpu.make_async_copy(got, got, f_recv).wait()
     for q in range(1, owners):
         router_across(q).start()
-    for d in range(1, n):
-        router_copy(d).wait_send()
+    sent = orouter.at[rrows, pl.ds(0, half * rlen)]
+    pltpu.make_async_copy(sent, sent, r_send).wait()
+    pltpu.make_async_copy(got, got, f_send).wait()
     for m in range(2):
         block = outs[m].at[:, pl.ds(0, depth), :]
         pltpu.make_async_copy(block, block, own_sem.at[m]).wait()
@@ -366,7 +406,6 @@
     dma = pltpu.SemaphoreType.DMA
     hbm = pl.BlockSpec(memory_space=pl.ANY)
     vmem = pl.BlockSpec(memory_space=pltpu.VMEM)
-    smem = pl.BlockSpec(memory_space=pltpu.SMEM)
     landed = pl.pallas_call(
         functools.partial(kernel, n, owners),
         out_shape=(
@@ -376,11 +415,11 @@
             OUT((experts, cols), f32),
             OUT((owners * rexp, n * rlen), bf16),
         ),
-        in_specs=[hbm] * 4 + [smem, vmem, vmem],
+        in_specs=[hbm] * 7,
         out_specs=(OUT_SPEC, OUT_SPEC, vmem, vmem, vmem),
         scratch_shapes=[
             pltpu.VMEM((2, 4, depth, width), f32),
-            pltpu.VMEM((STAGES + 1, 2, depth, width), f32),
+            pltpu.VMEM((SLOTS, 2, depth, width), f32),
             pltpu.VMEM((experts, n // 2, 4, cols), f32),
             pltpu.VMEM((experts, n // 2 - 1, 4, cols), f32),
             pltpu.VMEM((experts, 4, cols), f32),
@@ -389,9 +428,12 @@
             pltpu.VMEM((experts, n // 2, 4, cols), f32),
             pltpu.VMEM((2, n, experts, depth, cols), bf16),
             pltpu.VMEM((rexp, rlen), bf16),
-            dma((2, 4)), dma((len(HEAD), 4)), dma, dma, dma, dma, dma, dma((experts,)), dma, dma((experts,)), dma, dma((experts,)),
+            pltpu.SMEM((experts,), f32),
+            pltpu.VMEM((rexp, rlen), f32),
+            pltpu.VMEM((1, rlen), f32),
+            dma((3,)), dma((2, 4)), dma((len(HEAD), 4)), dma, dma, dma, dma, dma, dma((experts,)), dma, dma((experts,)), dma, dma((experts,)),
             dma((2, n - 1)), dma((2, n - 1)), dma((2,)),
-            dma((n - 1,)), dma, dma((owners - 1,)), dma((owners - 1,)),
+            dma, dma((2,)), dma, dma, dma((owners - 1,)), dma((owners - 1,)),
         ],
         compiler_params=pltpu.CompilerParams(
             collective_id=0, has_side_effects=True, vmem_limit_bytes=LIMIT
@@ -410,7 +452,7 @@
 
 OUT = pltpu.VMEM
 OUT_SPEC = pl.BlockSpec(memory_space=pltpu.VMEM)
-LIMIT = 44 * 1024 * 1024
+LIMIT = 46 * 1024 * 1024
 
 
 def fits(mesh, w_gate, router_weight):
@@ -418,7 +460,7 @@
     experts, depth, width = w_gate.shape[0] // owners, w_gate.shape[1] // n, w_gate.shape[2]
     head = [depth // k for k in HEAD]
     half_raw = n // 2 * sum(head[:-1])
-    need = 4 * depth * width * (8 + 2 * (STAGES + 1)) + 4 * experts * depth * width
+    need = 4 * depth * width * (8 + 2 * SLOTS) + 4 * experts * depth * width
     return (
         n > 2 and owners > 1 and n & (n - 1) == 0 and owners & (owners - 1) == 0
         and width % (n * LANES) == 0 and depth % LANES == 0 and depth % STEP == 0

time: 378 us -> 375 us (level)
  no operation moved by 1% of the time
where the time goes in v2:
time: 375 us
  Pallas kernels  374 us (100%)
    pallas_call x1, Pallas kernels, body(): pl.pallas_call(functools.partial(kernel, n, owners), out_shape=(OUT((expe...  368 us

profile of v2, /device:TPU:0, one launch (start us, length us, event | category | flops | bytes accessed | tf_op | source)
XLA Modules:
  0.0 374.8 jit_solution(10053630743121264715)
XLA Ops:
  0.6 368.1 %shard_map.110 = (bf16[16,2048,128]{2,1,0:T(8,128)(2,1)S(1)}, bf16[16,2048,128]{2,1,0:T(8,128)(2,1)S(1)}, f32[16,128]{1,0:T(8,128)S(1)}, f32[16,128]{1,0:T(8,128)S(1)}, bf16[64,2048]{1,0:T(8,128)(2,1)S(1)}) custom-call(f32[16,256,1024]{2,1,0:T(8,128)} %wg.1, f32[16,256,1024]{2,1,0:T(8,128)} %ag.1, f32[16,256,1024]{2,1,0:T(8,128)} %wu.1, ...), custom_call_target="tpu_custom_call" | custom-call | tf_op jit(solution)/shard_map/pallas_call | solution.py:409
  368.8 6.0 %shard_map.111 = (bf16[16,2048,128]{2,1,0:T(8,128)(2,1)}, bf16[16,2048,128]{2,1,0:T(8,128)(2,1)}, f32[16,128]{1,0:T(8,128)}, f32[16,128]{1,0:T(8,128)}, bf16[64,2048]{1,0:T(8,128)(2,1)}) custom-call(bf16[16,2048,128]{2,1,0:T(8,128)(2,1)S(1)} %get-tuple-element.15.refs_0_, bf16[16,2048,128]{2,1,0:T(8,128)(2,1)S(1)} %get-tuple-element.16.refs_1_, ...), custom_call_target="tpu_custom_call" | custom-call | tf_op jit(solution)/shard_map/pallas_call | solution.py:442

commit v3 on v2

--- a/solution.py
+++ b/solution.py
@@ -13,7 +13,9 @@
 LEAD = 2
 STEP = 16
 PIECES = 4
-HEAD = (8, 8, 4, 2)
+HEAD = (8, 8, 8, 8, 2)
+INNER = (0, 1, 6, 6)
+OUTER = (6, 6, 7, 7)
 
 
 def plain(w_gate, avg_gate, w_up, avg_up, mix_share, router_weight, router_gain):
@@ -60,6 +62,7 @@
     top = 2 * (me // half)
     near = half * (me // half)
     far = half - near
+    inner = (me // half) != (2 * me // half) % 2
     raws = len(HEAD) - 1
     head = [depth // k for k in HEAD]
     edges = [sum(head[:p]) for p in range(len(head))]
@@ -195,10 +198,16 @@
             for copy in loads(i + 2, slot):
                 copy.start()
 
-    def ship(p):
-        for m in range(2):
-            for d in range(half, n):
-                raw_copy(p, m, d).start()
+    def ship(point):
+        for here, points in ((inner, INNER), (~inner, OUTER)):
+            parts = [p for p in range(raws) if points[p] == point]
+            if parts:
+                @pl.when(here)
+                def _():
+                    for p in parts:
+                        for m in range(2):
+                            for d in range(half, n):
+                                raw_copy(p, m, d).start()
 
     def spread(i):
         for d in range(half - 1, 0, -1):
@@ -291,8 +300,7 @@
 
         @pl.when(i == 1)
         def _():
-            for p in range(1, raws):
-                ship(p)
+            ship(len(HEAD) + 1)
             gate_rows()
             for d in range(half, 0, -1):
                 router_copy(d).start()
@@ -300,6 +308,10 @@
         @pl.when((i >= 2) & (i < LEAD + 2))
         def _():
             settle(i - 2)
+
+        @pl.when(i == 2)
+        def _():
+            ship(len(HEAD) + 2)
 
         @pl.when((i >= LEAD + 3) & (i <= experts + 2))
         def _():
@@ -335,10 +347,11 @@
             for copy in loads(1, 1):
                 copy.start()
             pl.semaphore_wait(barrier, n + owners - 2)
-            ship(0)
+        ship(p)
     for m in range(2):
         sums(0, m, accs[m])
     spread(0)
+    ship(len(HEAD))
     for copy in loads(2, 0):
         copy.start()
     lax.fori_loop(1, experts + 4, turn, 0)

time: 375 us -> 375 us (level)
  no operation moved by 1% of the time
where the time goes in v3:
time: 375 us
  Pallas kernels  374 us (100%)
    pallas_call x1, Pallas kernels, body(): pl.pallas_call(functools.partial(kernel, n, owners), out_shape=(OUT((expe...  368 us

profile of v3, /device:TPU:0, one launch (start us, length us, event | category | flops | bytes accessed | tf_op | source)
XLA Modules:
  0.0 374.6 jit_solution(13112131829604217179)
XLA Ops:
  0.6 368.0 %shard_map.110 = (bf16[16,2048,128]{2,1,0:T(8,128)(2,1)S(1)}, bf16[16,2048,128]{2,1,0:T(8,128)(2,1)S(1)}, f32[16,128]{1,0:T(8,128)S(1)}, f32[16,128]{1,0:T(8,128)S(1)}, bf16[64,2048]{1,0:T(8,128)(2,1)S(1)}) custom-call(f32[16,256,1024]{2,1,0:T(8,128)} %wg.1, f32[16,256,1024]{2,1,0:T(8,128)} %ag.1, f32[16,256,1024]{2,1,0:T(8,128)} %wu.1, ...), custom_call_target="tpu_custom_call" | custom-call | tf_op jit(solution)/shard_map/pallas_call | solution.py:422
  368.6 6.0 %shard_map.111 = (bf16[16,2048,128]{2,1,0:T(8,128)(2,1)}, bf16[16,2048,128]{2,1,0:T(8,128)(2,1)}, f32[16,128]{1,0:T(8,128)}, f32[16,128]{1,0:T(8,128)}, bf16[64,2048]{1,0:T(8,128)(2,1)}) custom-call(bf16[16,2048,128]{2,1,0:T(8,128)(2,1)S(1)} %get-tuple-element.15.refs_0_, bf16[16,2048,128]{2,1,0:T(8,128)(2,1)S(1)} %get-tuple-element.16.refs_1_, ...), custom_call_target="tpu_custom_call" | custom-call | tf_op jit(solution)/shard_map/pallas_call | solution.py:455
